TPU v7x, 512 devices: a whole 4x8x8 slice. The times are simulated.
512 devices in a mesh: section: 64 (over z, x, core), head: 8 (over y).
Axes of the slice: x: 4, y: 8, z: 8, core: 2. Of those that a mesh axis runs over, the one named last changes fastest.
Arguments:
- slice_rows: bfloat16 [8192, 4096], P('section', 'head'), may hold values from -6 to 6
- w_query: bfloat16 [4096, 4096], P(None, 'head'), may hold values from -0.09375 to 0.09375
- w_key: bfloat16 [4096, 1024], P(None, 'head'), may hold values from -0.09375 to 0.09375
- w_value: bfloat16 [4096, 1024], P(None, 'head'), may hold values from -0.09375 to 0.09375
- prefix_keys: bfloat16 [32768, 1024], P('section', 'head'), may hold values from -140 to 140
- prefix_values: bfloat16 [32768, 1024], P('section', 'head'), may hold values from -6 to 6
- prefix_blocks: int32 [64], replicated, may hold values from 1 to 2, as said below
Outputs:
- attention: bfloat16 [8192, 4096], P('section', 'head')
Inputs may be any that keep to these rules, and one draw needn't show every extreme that they name: `prefix_blocks`: every section holds at least one live block; in every draw some section holds 2 blocks.
All inputs are finite; a program needn't handle non-finite values.
Results may differ from a plain program's by a relative error of at most 0.012.
The roundings to bfloat16 on the way count: a program that leaves them out, or rounds other values in their place, can miss the bound.
Values may be sent and summed in bfloat16 or wider, within the bound.
A program may use at most 64 MiB of HBM per device.

v0:
```python
import math

import jax
import jax.numpy as jnp
from jax import lax
from jax.sharding import PartitionSpec as P

HEAD_DIM = 128
BLOCK = 256
REACH = 7


def in_order(blocks, dim):
    blocks = jnp.moveaxis(blocks, 0, dim)
    dims = blocks.shape
    return blocks.reshape(*dims[:dim], dims[dim] * dims[dim + 1], *dims[dim + 2 :])


def from_everyone(value, axis):
    peers = lax.axis_size(axis)
    return lax.all_to_all(
        jnp.broadcast_to(value[None], (peers, *value.shape)), axis, 0, 0, tiled=True
    )


def collect(value, axis, dim):
    return in_order(from_everyone(value, axis), dim)


def passed_along(value, axis, by):
    peers = lax.axis_size(axis)
    pairs = [(i, i + by) for i in range(peers) if 0 <= i + by < peers]
    return lax.ppermute(value, axis, pairs)


def attend(queries, key_rows, values, live_mask):
    factor = 1.0 / math.sqrt(queries.shape[-1])
    scores = (
        jnp.einsum("thge,khe->hgtk", queries, key_rows, preferred_element_type=jnp.float32) * factor
    )
    scores = jnp.where(live_mask, scores, -1e30)
    row_max = jnp.max(scores, axis=-1)
    weights = jnp.where(live_mask, jnp.exp(scores - row_max[..., None]), 0.0)
    totals = jnp.sum(weights, axis=-1)
    rounded = weights.astype(jnp.bfloat16)
    result = jnp.einsum("hgtk,khe->thge", rounded, values, preferred_element_type=jnp.float32)
    return (row_max, totals, result)


def spread_scale(factor):
    return jnp.moveaxis(factor, 2, 0)[..., None]


def combine(first_part, second_part):
    row_max = jnp.maximum(first_part[0], second_part[0])
    first_scale = jnp.exp(first_part[0] - row_max)
    second_scale = jnp.exp(second_part[0] - row_max)
    totals = first_part[1] * first_scale + second_part[1] * second_scale
    result = first_part[2] * spread_scale(first_scale) + second_part[2] * spread_scale(second_scale)
    return (row_max, totals, result)


def on_device(slice_rows, w_query, w_key, w_value, prefix_keys, prefix_values, prefix_blocks):
    row_count = slice_rows.shape[0]
    head_count = w_key.shape[1] // HEAD_DIM
    group_size = w_query.shape[1] // w_key.shape[1]
    projections = (w_query, w_key, w_value)
    column_block = collect(slice_rows, "head", 1)
    projected = tuple(
        (
            jnp.dot(column_block, weight, preferred_element_type=jnp.float32)
            for weight in projections
        )
    )
    queries = projected[0].astype(jnp.bfloat16)
    own_keys = projected[1].astype(jnp.bfloat16).reshape(row_count, head_count, HEAD_DIM)
    own_values = projected[2].astype(jnp.bfloat16).reshape(row_count, head_count, HEAD_DIM)
    local_q = queries.reshape(row_count, head_count, group_size, HEAD_DIM)
    prefix_len = prefix_keys.shape[0]
    section_count = prefix_blocks.shape[0]
    section_index = lax.axis_index("section")
    positions = jnp.arange(prefix_len)
    sections_all = jnp.arange(section_count)

    def live_of(offset):
        owner_section = section_index - offset
        blocks = jnp.sum(jnp.where(sections_all == owner_section, prefix_blocks, 0))
        return (positions < blocks * BLOCK)[None, :]

    causal = jnp.arange(row_count)[:, None] >= jnp.arange(row_count)[None, :]
    merged = attend(local_q, own_keys, own_values, causal)
    held_k = prefix_keys.reshape(prefix_len, head_count, HEAD_DIM)
    held_v = prefix_values.reshape(prefix_len, head_count, HEAD_DIM)
    own_live = live_of(0)
    merged = combine(merged, attend(local_q, held_k, held_v, own_live))
    carried = (prefix_keys, prefix_values)
    for offset in range(1, REACH + 1):
        carried = passed_along((carried[0], carried[1]), "section", 1)
        merged = combine(
            merged,
            attend(
                local_q,
                carried[0].reshape(prefix_len, head_count, HEAD_DIM),
                carried[1].reshape(prefix_len, head_count, HEAD_DIM),
                live_of(offset),
            ),
        )
    final = merged[2] / spread_scale(merged[1])
    return final.reshape(row_count, head_count * group_size * HEAD_DIM).astype(jnp.bfloat16)


def solution(mesh):
    in_specs = (
        P("section", "head"),
        P(None, "head"),
        P(None, "head"),
        P(None, "head"),
        P("section", "head"),
        P("section", "head"),
        P(),
    )
    out_specs = P("section", "head")
    return jax.shard_map(
        on_device, mesh=mesh, in_specs=in_specs, out_specs=out_specs, check_vma=False
    )
```

profile of v0, /device:TPU:207, one launch (start us, length us, event | category | flops | bytes accessed | tf_op | source)
XLA Modules:
  0.0 110.4 jit_solution(15911050224035845444)
XLA Ops:
  0.0 1.1 %copy.21 = bf16[128,512]{0,1:T(8,128)(2,1)S(1)} copy(bf16[128,512]{1,0:T(8,128)(2,1)} %param.7) | data formatting | bytes 262144 | tf_op args[0]
  1.1 1.1 %broadcast_in_dim.171 = bf16[8,128,512]{1,2,0:T(8,128)(2,1)} broadcast(bf16[128,512]{0,1:T(8,128)(2,1)S(1)} %copy.21), dimensions={1,2} | broadcast | bytes 1179648 | tf_op jit(solution)/shard_map/broadcast_in_dim | solution.py:22
  2.2 7.0 %all-to-all-start = ((bf16[8,128,512]{1,2,0:T(8,128)(2,1)}), bf16[8,128,512]{1,2,0:T(8,128)(2,1)S(1)}, u32[]{:S(2)}, u32[]{:S(2)}) async-start(bf16[8,128,512]{1,2,0:T(8,128)(2,1)} %broadcast_in_dim.171), calls=%async_computation | async-start | bytes 2097152 | tf_op jit(solution)/shard_map/all_to_all | solution.py:21
  9.2 6.4 %collective-permute-start = (bf16[512,128]{1,0:T(8,128)(2,1)}, bf16[512,128]{1,0:T(8,128)(2,1)S(1)}, u32[]{:S(2)}, u32[]{:S(2)}) collective-permute-start(bf16[512,128]{1,0:T(8,128)(2,1)} %param.11), channel_id=1, source_target_pairs={{0,8},{8,16},{16,24},{24,32},{32,40},{40,48},{48,56},{56,64},{64,7... | collective-permute-start | bytes 393224 | tf_op jit(solution)/shard_map/ppermute | solution.py:33
  15.6 1.0 copy.27
  16.6 1.9 %collective-permute-start.1 = (bf16[512,128]{0,1:T(8,128)(2,1)S(1)}, bf16[512,128]{0,1:T(8,128)(2,1)S(1)}, u32[]{:S(2)}, u32[]{:S(2)}) collective-permute-start(bf16[512,128]{0,1:T(8,128)(2,1)S(1)} %copy.27), channel_id=1, source_target_pairs={{0,8},{8,16},{16,24},{24,32},{32,40},{40,48},{48,56},{56,64},{64,7... | collective-permute-start | bytes 393224 | tf_op jit(solution)/shard_map/ppermute | solution.py:33
  18.6 6.8 %collective-permute-start.2 = (bf16[512,128]{1,0:T(8,128)(2,1)S(1)}, bf16[512,128]{1,0:T(8,128)(2,1)S(1)}, u32[]{:S(2)}, u32[]{:S(2)}) collective-permute-start(bf16[512,128]{1,0:T(8,128)(2,1)S(1)} %collective-permute-done), channel_id=1, source_target_pairs={{0,8},{8,16},{16,24},{24,32},{32,40},{40,48},{48,56},{56,64},{64,7... | collective-permute-start | bytes 393224 | tf_op jit(solution)/shard_map/ppermute | solution.py:33
  25.4 2.7 %collective-permute-start.3 = (bf16[512,128]{0,1:T(8,128)(2,1)S(1)}, bf16[512,128]{0,1:T(8,128)(2,1)S(1)}, u32[]{:S(2)}, u32[]{:S(2)}) collective-permute-start(bf16[512,128]{0,1:T(8,128)(2,1)S(1)} %collective-permute-done.1), channel_id=1, source_target_pairs={{0,8},{8,16},{16,24},{24,32},{32,40},{40,48},{48,56},{56,64},{64,7... | collective-permute-start | bytes 393224 | tf_op jit(solution)/shard_map/ppermute | solution.py:33
  28.2 1.5 %fusion.199 = (s32[]{:T(128)}, s32[]{:T(128)}, s32[]{:T(128)}, s32[]{:T(128)}, s32[]{:T(128)}, /*index=5*/s32[]{:T(128)}, s32[]{:T(128)}, s32[]{:T(128)}) fusion(s32[64]{0:T(128)} %param.13, s32[]{:T(128)S(6)} %sub.369, s32[]{:T(128)S(6)} %sub.359, s32[]{:T(128)S(6)} %sub.354, s32[]{:T(128)S(6)} %sub.349, s32[]{:T(128)S(6)} %sub.344, s32[]{:T(128)S(6)} %sub.339, ...), kind=kLoop, calls=%fused_computation.269 | loop fusion | flops 1528 | bytes 320 | tf_op jit(solution)/shard_map/reduce_sum | solution.py:87
  30.9 0.6 iota_compare_fusion.1
  31.5 3.6 %collective-permute-start.4 = (bf16[512,128]{1,0:T(8,128)(2,1)S(1)}, bf16[512,128]{1,0:T(8,128)(2,1)S(1)}, u32[]{:S(2)}, u32[]{:S(2)}) collective-permute-start(bf16[512,128]{1,0:T(8,128)(2,1)S(1)} %collective-permute-done.2), channel_id=1, source_target_pairs={{0,8},{8,16},{16,24},{24,32},{32,40},{40,48},{48,56},{56,64},{64,7... | collective-permute-start | bytes 393224 | tf_op jit(solution)/shard_map/ppermute | solution.py:33
  35.0 2.7 %collective-permute-start.5 = (bf16[512,128]{0,1:T(8,128)(2,1)S(1)}, bf16[512,128]{0,1:T(8,128)(2,1)S(1)}, u32[]{:S(2)}, u32[]{:S(2)}) collective-permute-start(bf16[512,128]{0,1:T(8,128)(2,1)S(1)} %collective-permute-done.3), channel_id=1, source_target_pairs={{0,8},{8,16},{16,24},{24,32},{32,40},{40,48},{48,56},{56,64},{64,7... | collective-permute-start | bytes 393224 | tf_op jit(solution)/shard_map/ppermute | solution.py:33
  37.7 0.5 iota_compare_fusion.2
  39.6 0.6 iota_compare_fusion.3
  40.2 4.4 %collective-permute-start.6 = (bf16[512,128]{1,0:T(8,128)(2,1)S(1)}, bf16[512,128]{1,0:T(8,128)(2,1)S(1)}, u32[]{:S(2)}, u32[]{:S(2)}) collective-permute-start(bf16[512,128]{1,0:T(8,128)(2,1)S(1)} %collective-permute-done.4), channel_id=1, source_target_pairs={{0,8},{8,16},{16,24},{24,32},{32,40},{40,48},{48,56},{56,64},{64,7... | collective-permute-start | bytes 393224 | tf_op jit(solution)/shard_map/ppermute | solution.py:33
  44.6 2.7 %collective-permute-start.7 = (bf16[512,128]{0,1:T(8,128)(2,1)S(1)}, bf16[512,128]{0,1:T(8,128)(2,1)S(1)}, u32[]{:S(2)}, u32[]{:S(2)}) collective-permute-start(bf16[512,128]{0,1:T(8,128)(2,1)S(1)} %collective-permute-done.5), channel_id=1, source_target_pairs={{0,8},{8,16},{16,24},{24,32},{32,40},{40,48},{48,56},{56,64},{64,7... | collective-permute-start | bytes 393224 | tf_op jit(solution)/shard_map/ppermute | solution.py:33
  47.3 0.6 iota_compare_fusion.4
  49.6 4.6 %collective-permute-start.8 = (bf16[512,128]{1,0:T(8,128)(2,1)S(1)}, bf16[512,128]{1,0:T(8,128)(2,1)S(1)}, u32[]{:S(2)}, u32[]{:S(2)}) collective-permute-start(bf16[512,128]{1,0:T(8,128)(2,1)S(1)} %collective-permute-done.6), channel_id=1, source_target_pairs={{0,8},{8,16},{16,24},{24,32},{32,40},{40,48},{48,56},{56,64},{64,7... | collective-permute-start | bytes 393224 | tf_op jit(solution)/shard_map/ppermute | solution.py:33
  54.2 2.7 %collective-permute-start.9 = (bf16[512,128]{0,1:T(8,128)(2,1)S(1)}, bf16[512,128]{0,1:T(8,128)(2,1)S(1)}, u32[]{:S(2)}, u32[]{:S(2)}) collective-permute-start(bf16[512,128]{0,1:T(8,128)(2,1)S(1)} %collective-permute-done.7), channel_id=1, source_target_pairs={{0,8},{8,16},{16,24},{24,32},{32,40},{40,48},{48,56},{56,64},{64,7... | collective-permute-start | bytes 393224 | tf_op jit(solution)/shard_map/ppermute | solution.py:33
  56.9 0.5 iota_compare_fusion.6
  58.7 0.6 iota_compare_fusion.7
  59.3 4.5 %collective-permute-start.10 = (bf16[512,128]{1,0:T(8,128)(2,1)S(1)}, bf16[512,128]{1,0:T(8,128)(2,1)}, u32[]{:S(2)}, u32[]{:S(2)}) collective-permute-start(bf16[512,128]{1,0:T(8,128)(2,1)S(1)} %collective-permute-done.8), channel_id=1, source_target_pairs={{0,8},{8,16},{16,24},{24,32},{32,40},{40,48},{48,56},{56,64},{64,7... | collective-permute-start | bytes 393224 | tf_op jit(solution)/shard_map/ppermute | solution.py:33
  63.8 2.7 %collective-permute-start.11 = (bf16[512,128]{0,1:T(8,128)(2,1)S(1)}, bf16[512,128]{0,1:T(8,128)(2,1)}, u32[]{:S(2)}, u32[]{:S(2)}) collective-permute-start(bf16[512,128]{0,1:T(8,128)(2,1)S(1)} %collective-permute-done.9), channel_id=1, source_target_pairs={{0,8},{8,16},{16,24},{24,32},{32,40},{40,48},{48,56},{56,64},{64,7... | collective-permute-start | bytes 393224 | tf_op jit(solution)/shard_map/ppermute | solution.py:33
  67.1 6.4 %collective-permute-start.12 = (bf16[512,128]{1,0:T(8,128)(2,1)}, bf16[512,128]{1,0:T(8,128)(2,1)}, u32[]{:S(2)}, u32[]{:S(2)}) collective-permute-start(bf16[512,128]{1,0:T(8,128)(2,1)} %collective-permute-done.10), channel_id=1, source_target_pairs={{0,8},{8,16},{16,24},{24,32},{32,40},{40,48},{48,56},{56,64},{64,7... | collective-permute-start | bytes 393224 | tf_op jit(solution)/shard_map/ppermute | solution.py:33
  73.5 2.7 %collective-permute-start.13 = (bf16[512,128]{0,1:T(8,128)(2,1)}, bf16[512,128]{0,1:T(8,128)(2,1)}, u32[]{:S(2)}, u32[]{:S(2)}) collective-permute-start(bf16[512,128]{0,1:T(8,128)(2,1)} %collective-permute-done.11), channel_id=1, source_target_pairs={{0,8},{8,16},{16,24},{24,32},{32,40},{40,48},{48,56},{56,64},{64,7... | collective-permute-start | bytes 393224 | tf_op jit(solution)/shard_map/ppermute | solution.py:33
  76.3 2.9 %fusion.52 = bf16[16,4,8,128]{3,2,1,0:T(8,128)(2,1)S(1)} fusion(bf16[128,4096]{0,1:T(8,128)(2,1)S(1)} %bitcast.641, bf16[4096,512]{1,0:T(8,128)(2,1)} %param.8), kind=kOutput, calls=%fused_computation.71 | convolution fusion | flops 536936448 | bytes 5373952 | tf_op jit(solution)/shard_map/dot_general | solution.py:71
  79.2 1.2 %fusion.219 = (f32[4,128]{1,0:T(4,128)}, f32[1,4,128,128]{2,3,1,0:T(8,128)S(1)}) fusion(bf16[16,4,8,128]{3,2,1,0:T(8,128)(2,1)S(1)} %fusion.52, bf16[128,4096]{0,1:T(8,128)(2,1)S(1)} %bitcast.642, bf16[4096,128]{1,0:T(8,128)(2,1)S(1)} %copy-done, pred[128,128]{0,1:T(8,128)(4,1)S(1)} %iota_compare_fusion), kind=kOutput, calls=%fused_computation.289 | convolution fusion | flops 151207424 | bytes 2508800 | tf_op jit(solution)/shard_map/thge,khe->hgtk/dot_general | solution.py:39
  80.5 1.0 fusion.218
  81.6 1.4 %fusion.212 = (f32[4,128]{1,0:T(4,128)S(1)}, f32[1,4,128,512]{3,2,1,0:T(8,128)S(1)}) fusion(bf16[512,128]{1,0:T(8,128)(2,1)} %collective-permute-done.12, bf16[16,4,8,128]{3,2,1,0:T(8,128)(2,1)S(1)} %fusion.52, pred[512]{0:T(512)(128)(4,1)} %iota_compare_fusion.1), kind=kOutput, calls=%fused_computation.282 | convolution fusion | flops 67894784 | bytes 1313280 | tf_op jit(solution)/shard_map/thge,khe->hgtk/dot_general | solution.py:39
  83.1 1.7 %fusion.69 = f32[4,128]{1,0:T(4,128)} fusion(f32[1,4,128,512]{3,2,1,0:T(8,128)S(1)} %get-tuple-element.43, f32[4,128]{1,0:T(4,128)S(1)} %get-tuple-element.42, pred[512]{0:T(512)(128)(4,1)} %iota_compare_fusion.1), kind=kLoop, calls=%fused_computation.98 | loop fusion | flops 785920 | bytes 1053184 | tf_op jit(solution)/shard_map/reduce_sum | solution.py:44
  84.8 1.3 %fusion.213 = (f32[4,128]{1,0:T(4,128)S(1)}, f32[1,4,128,512]{3,2,1,0:T(8,128)S(1)}) fusion(bf16[512,128]{1,0:T(8,128)(2,1)} %collective-permute-done.10, bf16[16,4,8,128]{3,2,1,0:T(8,128)(2,1)S(1)} %fusion.52, pred[512]{0:T(512)(128)(4,1)} %iota_compare_fusion.2), kind=kOutput, calls=%fused_computation.283 | convolution fusion | flops 67894784 | bytes 1313280 | tf_op jit(solution)/shard_map/thge,khe->hgtk/dot_general | solution.py:39
  86.1 0.9 fusion.67
  87.5 0.9 fusion.65
  88.8 0.9 fusion.63
  90.0 1.0 fusion.61
  91.4 0.9 fusion.59
  92.7 0.9 fusion.57
  93.6 0.6 fusion.200
  94.2 0.9 fusion.55
  95.2 0.7 fusion.111
  95.9 0.7 fusion.188
  96.6 2.5 %fusion.49 = f32[128,1,4,128]{0,3,2,1:T(8,128)} fusion(bf16[128,4096]{0,1:T(8,128)(2,1)S(1)} %bitcast.643, bf16[4096,128]{1,0:T(8,128)(2,1)} %param.10, f32[1,4,128,128]{2,3,1,0:T(8,128)S(1)} %get-tuple-element.57, f32[128,4]{0,1:T(4,128)} %get-tuple-element.36, f32[4,128]{1,0:T(4,128)} %get-tuple-element.56, pred[128,128]{0,1:T(8,128)(4,1)S(1)} %iota_compare_fusion), kind=kOutput, calls=%fused_computation.67 | convolution fusion | flops 151273472 | bytes 2641920 | tf_op jit(solution)/shard_map/hgtk,khe->thge/dot_general | solution.py:46
  99.3 1.9 %fusion.48 = f32[128,1,4,128]{0,3,2,1:T(8,128)S(1)} fusion(f32[128,1,4,128]{0,3,2,1:T(8,128)} %fusion.49, f32[1,4,128,512]{3,2,1,0:T(8,128)} %copy-done.5, f32[4,128]{1,0:T(4,128)} %copy-done.32, pred[512]{0:T(512)(128)(4,1)} %iota_compare_fusion.8, bf16[512,128]{1,0:T(8,128)(2,1)} %param.12, f32[128,4]{0,1:T(4,128)} %get-tuple-element.38, ...), kind=kOutput, calls=%fused_computation.66 | convolution fusion | flops 68091904 | bytes 1710592 | tf_op jit(solution)/shard_map/hgtk,khe->thge/dot_general | solution.py:46
  101.3 1.7 %fusion.47 = f32[128,1,4,128]{0,3,2,1:T(8,128)S(1)} fusion(f32[128,1,4,128]{0,3,2,1:T(8,128)S(1)} %fusion.48, f32[1,4,128,512]{3,2,1,0:T(8,128)} %copy-done.9, f32[4,128]{1,0:T(4,128)} %copy-done.44, pred[512]{0:T(512)(128)(4,1)} %iota_compare_fusion.7, bf16[512,128]{0,1:T(8,128)(2,1)S(1)} %copy-done.14, f32[128,4]{0,1:T(4,128)} %get-tuple-element.39, ...), kind=kOutput, calls=%fused_computation.65 | convolution fusion | flops 68091904 | bytes 1710592 | tf_op jit(solution)/shard_map/hgtk,khe->thge/dot_general | solution.py:46
  103.2 1.8 %fusion.46 = f32[128,1,4,128]{0,3,2,1:T(8,128)S(1)} fusion(f32[128,1,4,128]{0,3,2,1:T(8,128)S(1)} %fusion.47, f32[1,4,128,512]{3,2,1,0:T(8,128)} %copy-done.8, f32[4,128]{1,0:T(4,128)} %copy-done.42, pred[512]{0:T(512)(128)(4,1)} %iota_compare_fusion.6, bf16[512,128]{0,1:T(8,128)(2,1)} %copy-done.15, f32[128,4]{0,1:T(4,128)} %get-tuple-element.26, ...), kind=kOutput, calls=%fused_computation.64 | convolution fusion | flops 68091904 | bytes 1710592 | tf_op jit(solution)/shard_map/hgtk,khe->thge/dot_general | solution.py:46
  106.6 1.4 %fusion.42 = f32[128,1,4,128]{0,3,2,1:T(8,128)S(1)} fusion(f32[128,1,4,128]{0,3,2,1:T(8,128)S(1)} %fusion.43, f32[1,4,128,512]{3,2,1,0:T(8,128)S(1)} %get-tuple-element.45, f32[4,128]{1,0:T(4,128)S(1)} %copy-done.35, pred[512]{0:T(512)(128)(4,1)S(1)} %copy-done.72, bf16[512,128]{0,1:T(8,128)(2,1)} %collective-permute-done.11, f32[128,4]{0,1:T(4,128)S(1)} %copy-done.54, ...), kind=kOutput, calls=%fused_computation.60 | convolution fusion | flops 68091904 | bytes 1710592 | tf_op jit(solution)/shard_map/hgtk,khe->thge/dot_general | solution.py:46
  108.2 1.4 %fusion.50 = bf16[128,1,4,128]{0,3,2,1:T(8,128)(2,1)S(1)} fusion(f32[128,1,4,128]{0,3,2,1:T(8,128)S(1)} %fusion.42, f32[1,4,128,512]{3,2,1,0:T(8,128)S(1)} %copy-done.11, f32[4,128]{1,0:T(4,128)S(1)} %copy-done.49, pred[512]{0:T(512)(128)(4,1)S(1)} %copy-done.82, bf16[512,128]{0,1:T(8,128)(2,1)} %collective-permute-done.13, f32[128,4]{0,1:T(4,128)S(1)} %fusion.155, ...), kind=kOutput, calls=%fused_computation.69 | convolution fusion | flops 68157440 | bytes 1579520 | tf_op jit(solution)/shard_map/hgtk,khe->thge/dot_general | solution.py:46
  109.6 0.8 copy.34
  (195 shorter events, 4.7 us)
Async XLA Ops:
  0.0 79.2 %copy-start = (bf16[4096,128]{1,0:T(8,128)(2,1)S(1)}, bf16[4096,128]{1,0:T(8,128)(2,1)}, u32[]{:S(2)}) copy-start(bf16[4096,128]{1,0:T(8,128)(2,1)} %param.9) | copy-start | bytes 3145732
  2.2 74.0 %all-to-all-start = ((bf16[8,128,512]{1,2,0:T(8,128)(2,1)}), bf16[8,128,512]{1,2,0:T(8,128)(2,1)S(1)}, u32[]{:S(2)}, u32[]{:S(2)}) async-start(bf16[8,128,512]{1,2,0:T(8,128)(2,1)} %broadcast_in_dim.171), calls=%async_computation | async-start | bytes 2097152 | tf_op jit(solution)/shard_map/all_to_all | solution.py:21
  9.2 71.2 %copy-start.12 = (bf16[512,128]{1,0:T(8,128)(2,1)S(1)}, bf16[512,128]{1,0:T(8,128)(2,1)}, u32[]{:S(2)}) copy-start(bf16[512,128]{1,0:T(8,128)(2,1)} %param.11) | copy-start | bytes 393220
  9.2 9.3 %collective-permute-start = (bf16[512,128]{1,0:T(8,128)(2,1)}, bf16[512,128]{1,0:T(8,128)(2,1)S(1)}, u32[]{:S(2)}, u32[]{:S(2)}) collective-permute-start(bf16[512,128]{1,0:T(8,128)(2,1)} %param.11), channel_id=1, source_target_pairs={{0,8},{8,16},{16,24},{24,32},{32,40},{40,48},{48,56},{56,64},{64,7... | collective-permute-start | bytes 393224 | tf_op jit(solution)/shard_map/ppermute | solution.py:33
  16.6 8.8 %collective-permute-start.1 = (bf16[512,128]{0,1:T(8,128)(2,1)S(1)}, bf16[512,128]{0,1:T(8,128)(2,1)S(1)}, u32[]{:S(2)}, u32[]{:S(2)}) collective-permute-start(bf16[512,128]{0,1:T(8,128)(2,1)S(1)} %copy.27), channel_id=1, source_target_pairs={{0,8},{8,16},{16,24},{24,32},{32,40},{40,48},{48,56},{56,64},{64,7... | collective-permute-start | bytes 393224 | tf_op jit(solution)/shard_map/ppermute | solution.py:33
  18.6 62.9 %copy-start.16 = (bf16[512,128]{1,0:T(8,128)(2,1)}, bf16[512,128]{1,0:T(8,128)(2,1)S(1)}, u32[]{:S(2)}) copy-start(bf16[512,128]{1,0:T(8,128)(2,1)S(1)} %collective-permute-done) | copy-start | bytes 393220
  18.6 12.9 %collective-permute-start.2 = (bf16[512,128]{1,0:T(8,128)(2,1)S(1)}, bf16[512,128]{1,0:T(8,128)(2,1)S(1)}, u32[]{:S(2)}, u32[]{:S(2)}) collective-permute-start(bf16[512,128]{1,0:T(8,128)(2,1)S(1)} %collective-permute-done), channel_id=1, source_target_pairs={{0,8},{8,16},{16,24},{24,32},{32,40},{40,48},{48,56},{56,64},{64,7... | collective-permute-start | bytes 393224 | tf_op jit(solution)/shard_map/ppermute | solution.py:33
  25.4 56.1 %copy-start.13 = (bf16[512,128]{0,1:T(8,128)(2,1)}, bf16[512,128]{0,1:T(8,128)(2,1)S(1)}, u32[]{:S(2)}) copy-start(bf16[512,128]{0,1:T(8,128)(2,1)S(1)} %collective-permute-done.1) | copy-start | bytes 393220
  25.4 9.6 %collective-permute-start.3 = (bf16[512,128]{0,1:T(8,128)(2,1)S(1)}, bf16[512,128]{0,1:T(8,128)(2,1)S(1)}, u32[]{:S(2)}, u32[]{:S(2)}) collective-permute-start(bf16[512,128]{0,1:T(8,128)(2,1)S(1)} %collective-permute-done.1), channel_id=1, source_target_pairs={{0,8},{8,16},{16,24},{24,32},{32,40},{40,48},{48,56},{56,64},{64,7... | collective-permute-start | bytes 393224 | tf_op jit(solution)/shard_map/ppermute | solution.py:33
  31.5 50.1 %copy-start.20 = (bf16[512,128]{1,0:T(8,128)(2,1)}, bf16[512,128]{1,0:T(8,128)(2,1)S(1)}, u32[]{:S(2)}) copy-start(bf16[512,128]{1,0:T(8,128)(2,1)S(1)} %collective-permute-done.2) | copy-start | bytes 393220
  31.5 8.7 %collective-permute-start.4 = (bf16[512,128]{1,0:T(8,128)(2,1)S(1)}, bf16[512,128]{1,0:T(8,128)(2,1)S(1)}, u32[]{:S(2)}, u32[]{:S(2)}) collective-permute-start(bf16[512,128]{1,0:T(8,128)(2,1)S(1)} %collective-permute-done.2), channel_id=1, source_target_pairs={{0,8},{8,16},{16,24},{24,32},{32,40},{40,48},{48,56},{56,64},{64,7... | collective-permute-start | bytes 393224 | tf_op jit(solution)/shard_map/ppermute | solution.py:33
  35.0 46.5 %copy-start.15 = (bf16[512,128]{0,1:T(8,128)(2,1)}, bf16[512,128]{0,1:T(8,128)(2,1)S(1)}, u32[]{:S(2)}) copy-start(bf16[512,128]{0,1:T(8,128)(2,1)S(1)} %collective-permute-done.3) | copy-start | bytes 393220
  35.0 9.6 %collective-permute-start.5 = (bf16[512,128]{0,1:T(8,128)(2,1)S(1)}, bf16[512,128]{0,1:T(8,128)(2,1)S(1)}, u32[]{:S(2)}, u32[]{:S(2)}) collective-permute-start(bf16[512,128]{0,1:T(8,128)(2,1)S(1)} %collective-permute-done.3), channel_id=1, source_target_pairs={{0,8},{8,16},{16,24},{24,32},{32,40},{40,48},{48,56},{56,64},{64,7... | collective-permute-start | bytes 393224 | tf_op jit(solution)/shard_map/ppermute | solution.py:33
  40.2 14.0 %copy-start.26 = (bf16[512,128]{1,0:T(8,128)(2,1)}, bf16[512,128]{1,0:T(8,128)(2,1)S(1)}, u32[]{:S(2)}) copy-start(bf16[512,128]{1,0:T(8,128)(2,1)S(1)} %collective-permute-done.4) | copy-start | bytes 393220
  40.2 9.4 %collective-permute-start.6 = (bf16[512,128]{1,0:T(8,128)(2,1)S(1)}, bf16[512,128]{1,0:T(8,128)(2,1)S(1)}, u32[]{:S(2)}, u32[]{:S(2)}) collective-permute-start(bf16[512,128]{1,0:T(8,128)(2,1)S(1)} %collective-permute-done.4), channel_id=1, source_target_pairs={{0,8},{8,16},{16,24},{24,32},{32,40},{40,48},{48,56},{56,64},{64,7... | collective-permute-start | bytes 393224 | tf_op jit(solution)/shard_map/ppermute | solution.py:33
  44.6 36.9 %copy-start.18 = (bf16[512,128]{0,1:T(8,128)(2,1)}, bf16[512,128]{0,1:T(8,128)(2,1)S(1)}, u32[]{:S(2)}) copy-start(bf16[512,128]{0,1:T(8,128)(2,1)S(1)} %collective-permute-done.5) | copy-start | bytes 393220
  44.6 9.6 %collective-permute-start.7 = (bf16[512,128]{0,1:T(8,128)(2,1)S(1)}, bf16[512,128]{0,1:T(8,128)(2,1)S(1)}, u32[]{:S(2)}, u32[]{:S(2)}) collective-permute-start(bf16[512,128]{0,1:T(8,128)(2,1)S(1)} %collective-permute-done.5), channel_id=1, source_target_pairs={{0,8},{8,16},{16,24},{24,32},{32,40},{40,48},{48,56},{56,64},{64,7... | collective-permute-start | bytes 393224 | tf_op jit(solution)/shard_map/ppermute | solution.py:33
  49.6 26.7 %copy-start.28 = (bf16[512,128]{1,0:T(8,128)(2,1)}, bf16[512,128]{1,0:T(8,128)(2,1)S(1)}, u32[]{:S(2)}) copy-start(bf16[512,128]{1,0:T(8,128)(2,1)S(1)} %collective-permute-done.6) | copy-start | bytes 393220
  49.6 9.7 %collective-permute-start.8 = (bf16[512,128]{1,0:T(8,128)(2,1)S(1)}, bf16[512,128]{1,0:T(8,128)(2,1)S(1)}, u32[]{:S(2)}, u32[]{:S(2)}) collective-permute-start(bf16[512,128]{1,0:T(8,128)(2,1)S(1)} %collective-permute-done.6), channel_id=1, source_target_pairs={{0,8},{8,16},{16,24},{24,32},{32,40},{40,48},{48,56},{56,64},{64,7... | collective-permute-start | bytes 393224 | tf_op jit(solution)/shard_map/ppermute | solution.py:33
  54.2 27.3 %copy-start.22 = (bf16[512,128]{0,1:T(8,128)(2,1)}, bf16[512,128]{0,1:T(8,128)(2,1)S(1)}, u32[]{:S(2)}) copy-start(bf16[512,128]{0,1:T(8,128)(2,1)S(1)} %collective-permute-done.7) | copy-start | bytes 393220
  54.2 9.6 %collective-permute-start.9 = (bf16[512,128]{0,1:T(8,128)(2,1)S(1)}, bf16[512,128]{0,1:T(8,128)(2,1)S(1)}, u32[]{:S(2)}, u32[]{:S(2)}) collective-permute-start(bf16[512,128]{0,1:T(8,128)(2,1)S(1)} %collective-permute-done.7), channel_id=1, source_target_pairs={{0,8},{8,16},{16,24},{24,32},{32,40},{40,48},{48,56},{56,64},{64,7... | collective-permute-start | bytes 393224 | tf_op jit(solution)/shard_map/ppermute | solution.py:33
  59.3 16.9 %copy-start.30 = (bf16[512,128]{1,0:T(8,128)(2,1)}, bf16[512,128]{1,0:T(8,128)(2,1)S(1)}, u32[]{:S(2)}) copy-start(bf16[512,128]{1,0:T(8,128)(2,1)S(1)} %collective-permute-done.8) | copy-start | bytes 393220
  59.3 7.7 %collective-permute-start.10 = (bf16[512,128]{1,0:T(8,128)(2,1)S(1)}, bf16[512,128]{1,0:T(8,128)(2,1)}, u32[]{:S(2)}, u32[]{:S(2)}) collective-permute-start(bf16[512,128]{1,0:T(8,128)(2,1)S(1)} %collective-permute-done.8), channel_id=1, source_target_pairs={{0,8},{8,16},{16,24},{24,32},{32,40},{40,48},{48,56},{56,64},{64,7... | collective-permute-start | bytes 393224 | tf_op jit(solution)/shard_map/ppermute | solution.py:33
  63.8 17.7 %copy-start.24 = (bf16[512,128]{0,1:T(8,128)(2,1)}, bf16[512,128]{0,1:T(8,128)(2,1)S(1)}, u32[]{:S(2)}) copy-start(bf16[512,128]{0,1:T(8,128)(2,1)S(1)} %collective-permute-done.9) | copy-start | bytes 393220
  63.8 9.7 %collective-permute-start.11 = (bf16[512,128]{0,1:T(8,128)(2,1)S(1)}, bf16[512,128]{0,1:T(8,128)(2,1)}, u32[]{:S(2)}, u32[]{:S(2)}) collective-permute-start(bf16[512,128]{0,1:T(8,128)(2,1)S(1)} %collective-permute-done.9), channel_id=1, source_target_pairs={{0,8},{8,16},{16,24},{24,32},{32,40},{40,48},{48,56},{56,64},{64,7... | collective-permute-start | bytes 393224 | tf_op jit(solution)/shard_map/ppermute | solution.py:33
  67.1 14.5 %collective-permute-start.12 = (bf16[512,128]{1,0:T(8,128)(2,1)}, bf16[512,128]{1,0:T(8,128)(2,1)}, u32[]{:S(2)}, u32[]{:S(2)}) collective-permute-start(bf16[512,128]{1,0:T(8,128)(2,1)} %collective-permute-done.10), channel_id=1, source_target_pairs={{0,8},{8,16},{16,24},{24,32},{32,40},{40,48},{48,56},{56,64},{64,7... | collective-permute-start | bytes 393224 | tf_op jit(solution)/shard_map/ppermute | solution.py:33
  73.5 34.6 %collective-permute-start.13 = (bf16[512,128]{0,1:T(8,128)(2,1)}, bf16[512,128]{0,1:T(8,128)(2,1)}, u32[]{:S(2)}, u32[]{:S(2)}) collective-permute-start(bf16[512,128]{0,1:T(8,128)(2,1)} %collective-permute-done.11), channel_id=1, source_target_pairs={{0,8},{8,16},{16,24},{24,32},{32,40},{40,48},{48,56},{56,64},{64,7... | collective-permute-start | bytes 393224 | tf_op jit(solution)/shard_map/ppermute | solution.py:33
  80.4 6.6 %copy-start.31 = (bf16[512,128]{1,0:T(8,128)(2,1)S(1)}, bf16[512,128]{1,0:T(8,128)(2,1)}, u32[]{:S(2)}) copy-start(bf16[512,128]{1,0:T(8,128)(2,1)} %copy-done.30) | copy-start | bytes 393220
  80.4 6.6 %copy-start.73 = (pred[512]{0:T(512)(128)(4,1)S(1)}, pred[512]{0:T(512)(128)(4,1)}, u32[]{:S(2)}) copy-start(pred[512]{0:T(512)(128)(4,1)} %iota_compare_fusion.3) | copy-start | bytes 1540
  80.5 7.9 %copy-start.29 = (bf16[512,128]{1,0:T(8,128)(2,1)S(1)}, bf16[512,128]{1,0:T(8,128)(2,1)}, u32[]{:S(2)}) copy-start(bf16[512,128]{1,0:T(8,128)(2,1)} %copy-done.28) | copy-start | bytes 393220
  80.5 7.9 %copy-start.75 = (pred[512]{0:T(512)(128)(4,1)S(1)}, pred[512]{0:T(512)(128)(4,1)}, u32[]{:S(2)}) copy-start(pred[512]{0:T(512)(128)(4,1)} %iota_compare_fusion.4) | copy-start | bytes 1540
  81.6 12.7 %copy-start.5 = (f32[1,4,128,512]{3,2,1,0:T(8,128)}, f32[1,4,128,512]{3,2,1,0:T(8,128)S(1)}, u32[]{:S(2)}) copy-start(f32[1,4,128,512]{3,2,1,0:T(8,128)S(1)} %get-tuple-element.55) | copy-start | bytes 3145732
  81.6 14.2 %copy-start.32 = (f32[4,128]{1,0:T(4,128)}, f32[4,128]{1,0:T(4,128)S(1)}, u32[]{:S(2)}) copy-start(f32[4,128]{1,0:T(4,128)S(1)} %get-tuple-element.54) | copy-start | bytes 6148
  83.1 12.8 %copy-start.48 = (f32[4,128]{1,0:T(4,128)}, f32[4,128]{1,0:T(4,128)S(1)}, u32[]{:S(2)}) copy-start(f32[4,128]{1,0:T(4,128)S(1)} %get-tuple-element.42) | copy-start | bytes 6148
  83.1 6.6 %copy-start.27 = (bf16[512,128]{1,0:T(8,128)(2,1)S(1)}, bf16[512,128]{1,0:T(8,128)(2,1)}, u32[]{:S(2)}) copy-start(bf16[512,128]{1,0:T(8,128)(2,1)} %copy-done.26) | copy-start | bytes 393220
  83.1 6.6 %copy-start.77 = (pred[512]{0:T(512)(128)(4,1)S(1)}, pred[512]{0:T(512)(128)(4,1)}, u32[]{:S(2)}) copy-start(pred[512]{0:T(512)(128)(4,1)} %iota_compare_fusion.5) | copy-start | bytes 1540
  86.1 9.7 %copy-start.34 = (f32[4,128]{1,0:T(4,128)}, f32[4,128]{1,0:T(4,128)S(1)}, u32[]{:S(2)}) copy-start(f32[4,128]{1,0:T(4,128)S(1)} %get-tuple-element.44) | copy-start | bytes 6148
  87.4 8.4 %copy-start.36 = (f32[4,128]{1,0:T(4,128)}, f32[4,128]{1,0:T(4,128)S(1)}, u32[]{:S(2)}) copy-start(f32[4,128]{1,0:T(4,128)S(1)} %get-tuple-element.46) | copy-start | bytes 6148
  88.7 6.4 %copy-start.3 = (f32[1,4,128,512]{3,2,1,0:T(8,128)}, f32[1,4,128,512]{3,2,1,0:T(8,128)S(1)}, u32[]{:S(2)}) copy-start(f32[1,4,128,512]{3,2,1,0:T(8,128)S(1)} %get-tuple-element.49) | copy-start | bytes 3145732
  88.7 7.1 %copy-start.38 = (f32[4,128]{1,0:T(4,128)}, f32[4,128]{1,0:T(4,128)S(1)}, u32[]{:S(2)}) copy-start(f32[4,128]{1,0:T(4,128)S(1)} %get-tuple-element.48) | copy-start | bytes 6148
  90.0 6.5 %copy-start.40 = (f32[4,128]{1,0:T(4,128)}, f32[4,128]{1,0:T(4,128)S(1)}, u32[]{:S(2)}) copy-start(f32[4,128]{1,0:T(4,128)S(1)} %get-tuple-element.40) | copy-start | bytes 6148
  92.7 8.5 %copy-start.14 = (bf16[512,128]{0,1:T(8,128)(2,1)S(1)}, bf16[512,128]{0,1:T(8,128)(2,1)}, u32[]{:S(2)}) copy-start(bf16[512,128]{0,1:T(8,128)(2,1)} %copy-done.13) | copy-start | bytes 393220
  99.2 6.8 %copy-start.2 = (f32[1,4,128,512]{3,2,1,0:T(8,128)S(1)}, f32[1,4,128,512]{3,2,1,0:T(8,128)}, u32[]{:S(2)}) copy-start(f32[1,4,128,512]{3,2,1,0:T(8,128)} %copy-done.1) | copy-start | bytes 3145732
  99.2 6.8 %copy-start.25 = (bf16[512,128]{0,1:T(8,128)(2,1)S(1)}, bf16[512,128]{0,1:T(8,128)(2,1)}, u32[]{:S(2)}) copy-start(bf16[512,128]{0,1:T(8,128)(2,1)} %copy-done.24) | copy-start | bytes 393220
  99.2 6.8 %copy-start.37 = (f32[4,128]{1,0:T(4,128)S(1)}, f32[4,128]{1,0:T(4,128)}, u32[]{:S(2)}) copy-start(f32[4,128]{1,0:T(4,128)} %copy-done.36) | copy-start | bytes 6148
  99.2 6.8 %copy-start.56 = (f32[128,4]{0,1:T(4,128)S(1)}, f32[128,4]{0,1:T(4,128)}, u32[]{:S(2)}) copy-start(f32[128,4]{0,1:T(4,128)} %get-tuple-element.29) | copy-start | bytes 6148
  99.3 6.8 %copy-start.57 = (f32[128,4]{0,1:T(4,128)S(1)}, f32[128,4]{0,1:T(4,128)}, u32[]{:S(2)}) copy-start(f32[128,4]{0,1:T(4,128)} %get-tuple-element.31) | copy-start | bytes 6148
  99.3 6.8 %copy-start.74 = (pred[512]{0:T(512)(128)(4,1)S(1)}, pred[512]{0:T(512)(128)(4,1)}, u32[]{:S(2)}) copy-start(pred[512]{0:T(512)(128)(4,1)} %iota_compare_fusion.3) | copy-start | bytes 1540
  (51 other events, 259.2 us)
where the time goes:
time: 111 us; the launch traced here: 110 us
  starting transfers between devices  61.8 us (56%)
  matrix products  21.9 us (20%)
  other arithmetic  15.9 us (14%)
  between operations  6.39 us (6%)
  local copies, waits for them, and re-layouts  4.36 us (4%)
    ppermute x14, starting transfers between devices, passed_along(): return lax.ppermute(value, axis, pairs)  54.8 us
    dot_general x9, matrix products, attend(): jnp.einsum('hgtk,khe->thge', rounded, values, preferred_element_type=jnp....  12.1 us
    reduce_sum x9, other arithmetic, attend(): totals = jnp.sum(weights, axis=-1)  8.7 us
    all_to_all x1, starting transfers between devices, from_everyone(): lax.all_to_all(jnp.broadcast_to(value[None], (peers, *value.shape)), axis...  6.99 us
    dot_general x9, matrix products, attend(): jnp.einsum('thge,khe->hgtk', queries, key_rows, preferred_element_type=jn...  6.87 us
    lt x8, other arithmetic, live_of(): return (positions < blocks * BLOCK)[None, :]  4.42 us
    dot_general x1, matrix products, on_device(): jnp.dot(column_block, weight, preferred_element_type=jnp.float32)  2.94 us
    unnamed x170, local copies, waits for them, and re-layouts  2.46 us
  transfers between devices with their start and end apart: 15, of which 0 were waited for; matrix products, arithmetic and copies ran while one was open for 34% of the time, Pallas kernels for 0%

commit v1 on v0

v1 whole, which is shorter than its diff:
```python
import functools
import math

import jax
import jax.numpy as jnp
from jax import lax
from jax.experimental import pallas as pl
from jax.experimental.pallas import tpu as pltpu
from jax.sharding import PartitionSpec as P

HEAD_DIM = 128
BLOCK = 256
REACH = 7
COLUMNS = 4
LAYERS = 8
RING = 8
HALF = 64
MESH = pl.DeviceIdType.MESH

DIRECT = [4.2, 5.6, 7.0, 8.4]
ALONE = [3.5, 4.2, 4.9, 5.6]
SECOND = [7.3, 8.7, 10.1, 11.5]
THIRD = [10.4, 11.8, 13.2, 14.6]
LOW_FIRST = [0, 1, 2, 3]
HIGH_FIRST = [2, 3, 0, 1]
LOW, HIGH = (0, 1), (2, 3)


def rows_of(piece):
    return pl.ds((piece // 2) * BLOCK, BLOCK)


def arrivals(column):
    events = []

    def add(times, slot, order, right=(), left=(), up=(), pass_on="both"):
        for time, piece in zip(times, order):
            events.append((time, slot, piece, piece in right, piece in left, piece in up, pass_on))

    every = LOW + HIGH
    if column == 0:
        add(ALONE, 0, LOW_FIRST, pass_on="own")
        add(DIRECT, "relay", LOW_FIRST, up=every, pass_on="none")
        add(SECOND, 1, LOW_FIRST)
        add(SECOND, 3, LOW_FIRST, right=LOW)
        add(THIRD, 2, LOW_FIRST)
    elif column == 1:
        add(ALONE, 1, LOW_FIRST, pass_on="own")
        add(DIRECT, 0, LOW_FIRST, right=LOW)
        add(DIRECT, "relay", LOW_FIRST, up=every, pass_on="none")
        add(SECOND, 2, LOW_FIRST, left=every)
        add(THIRD[:2], 3, LOW)
        add(THIRD[:2], 3, HIGH)
    elif column == 2:
        add(ALONE, 2, LOW_FIRST, pass_on="own")
        add(DIRECT, 1, LOW_FIRST, right=every)
        add(DIRECT, "relay", HIGH_FIRST, up=every, pass_on="none")
        add(SECOND, 3, HIGH_FIRST, left=HIGH)
        add([8.7, 10.1], 0, LOW)
        add([8.7, 10.1], 0, HIGH)
    else:
        add(DIRECT, 3, LOW_FIRST, right=every, pass_on="own_wait")
        add(DIRECT, 2, LOW_FIRST)
        add(DIRECT, 0, HIGH_FIRST, left=HIGH)
        add([8.7, 10.1, 11.5, 12.9], 1, LOW_FIRST)
    return sorted(events, key=lambda event: event[0])


def gather_kernel(
    x_ref, wq_ref, wk_ref, wv_ref, pk_ref, pv_ref,
    q_ref, k_ref, v_ref, kv_ref,
    xbuf, wq, wk, wv, acc, relay,
    w_sem, local_sem, x_send, x_recv,
    right_send, left_send, up_send, relay_send, right_fwd, left_fwd, pair_send,
    slot_recv, relay_recv, pair_recv,
):
    section = lax.axis_index("section")
    y = lax.axis_index("head")
    core = lax.rem(section, 2)
    x = lax.rem(lax.div(section, 2), COLUMNS)
    z = lax.div(section, 2 * COLUMNS)

    def section_at(layer, column, kind):
        return (layer * COLUMNS + column) * 2 + kind

    right = section_at(z, lax.rem(x + 1, COLUMNS), core)
    left = section_at(z, lax.rem(x + COLUMNS - 1, COLUMNS), core)
    above = section_at(lax.rem(z + 1, LAYERS), x, core)
    below = section_at(lax.rem(z + LAYERS - 1, LAYERS), x, core)
    pair = section_at(z, x, 1 - core)
    y_up = lax.rem(y + 1, RING)
    y_down = lax.rem(y + RING - 1, RING)

    def block_at(hop):
        return lax.rem(y + hop + RING, RING)

    visits = [0, -1, 1, -2, 2, -3, 3, 4]

    def weight_copies(hop):
        start = pl.multiple_of(block_at(hop) * 512, 512)
        rows = pl.ds(start, 512)
        at = visits.index(hop)
        return [
            pltpu.make_async_copy(source.at[rows], target.at[rows], w_sem.at[at, index])
            for index, (source, target) in enumerate(((wq_ref, wq), (wk_ref, wk), (wv_ref, wv)))
        ]

    own_x = pltpu.make_async_copy(x_ref, xbuf.at[y], local_sem.at[0])
    own_x.start()
    for copy in weight_copies(0):
        copy.start()

    barrier = pltpu.get_barrier_semaphore()
    for peer in (right, left, above, below, pair):
        pl.semaphore_signal(barrier, inc=1, device_id=(peer, y), device_id_type=MESH)
    for peer in (y_up, y_down):
        pl.semaphore_signal(barrier, inc=1, device_id=(section, peer), device_id_type=MESH)
    for hop in visits[1:]:
        for copy in weight_copies(hop):
            copy.start()
    own_k = pltpu.make_async_copy(pk_ref, kv_ref.at[8, 0], local_sem.at[1])
    own_v = pltpu.make_async_copy(pv_ref, kv_ref.at[8, 1], local_sem.at[2])
    own_k.start()
    own_v.start()
    pl.semaphore_wait(barrier, 7)

    def remote(source, target, send, recv, device):
        return pltpu.make_async_remote_copy(
            src_ref=source, dst_ref=target, send_sem=send, recv_sem=recv,
            device_id=device, device_id_type=MESH,
        )

    def x_copy(way, hop, half):
        origin = block_at(-hop if way == 0 else hop)
        rows = pl.ds(half * HALF, HALF)
        source = x_ref.at[rows] if hop == 0 else xbuf.at[origin, rows]
        return remote(
            source, xbuf.at[origin, rows],
            x_send.at[way, hop * 2 + half], x_recv.at[way, hop * 2 + half],
            (section, y_up if way == 0 else y_down),
        )

    def x_arrival(way, hop, half):
        origin = block_at(-hop - 1 if way == 0 else hop + 1)
        rows = pl.ds(half * HALF, HALF)
        return remote(
            xbuf.at[origin, rows], xbuf.at[origin, rows],
            x_send.at[way, hop * 2 + half], x_recv.at[way, hop * 2 + half],
            (section, y_up if way == 0 else y_down),
        )

    def x_sent(way, hop, half):
        return hop < 3 or half == way

    def own_piece(piece):
        return (pk_ref if piece % 2 == 0 else pv_ref).at[rows_of(piece)]

    def slot_piece(column, kind, piece):
        return kv_ref.at[column * 2 + kind, piece % 2, rows_of(piece)]

    def relay_piece(piece):
        return relay.at[piece % 2, rows_of(piece)]

    def send_right(piece):
        return remote(
            own_piece(piece), slot_piece(x, core, piece),
            right_send.at[piece], slot_recv.at[x, piece], (right, y),
        )

    def send_left(piece, column):
        if column == 0:
            return remote(
                own_piece(piece), slot_piece(0, core, piece),
                left_send.at[piece], slot_recv.at[0, piece], (left, y),
            )
        return remote(
            own_piece(piece), relay_piece(piece),
            left_send.at[piece], relay_recv.at[piece], (left, y),
        )

    def send_up(piece):
        return remote(
            own_piece(piece), slot_piece(x, core, piece),
            up_send.at[piece], slot_recv.at[x, piece], (above, y),
        )

    def send_relay(piece, column):
        return remote(
            relay_piece(piece), slot_piece(column + 1, core, piece),
            relay_send.at[piece], slot_recv.at[column + 1, piece], (above, y),
        )

    def forward(slot, piece, to_right):
        return remote(
            slot_piece(slot, core, piece), slot_piece(slot, core, piece),
            (right_fwd if to_right else left_fwd).at[piece], slot_recv.at[slot, piece],
            (right if to_right else left, y),
        )

    def hand_over(slot, piece):
        return remote(
            slot_piece(slot, core, piece), slot_piece(slot, core, piece),
            pair_send.at[slot, piece], pair_recv.at[slot, piece], (pair, y),
        )

    def hand_own(piece):
        return remote(
            own_piece(piece), slot_piece(x, 0, piece),
            pair_send.at[x, piece], pair_recv.at[x, piece], (pair, y),
        )

    for half in range(2):
        for way in range(2):
            x_copy(way, 0, half).start()
    for column in range(COLUMNS):

        @pl.when(x == column)
        def _():
            order = HIGH_FIRST if column in (0, 3) else LOW_FIRST
            for index in range(4):
                send_left(order[index], column).start()
                if column < 3:
                    send_right(index).start()
                else:
                    send_up(index).start()

    @pl.when((core == 1) & (x < 3))
    def _():
        for piece in range(4):
            send_up(piece).start()

    @pl.when(core == 0)
    def _():
        for piece in range(4):
            hand_own(piece).start()

    def handle(column, event):
        _, slot, piece, to_right, to_left, to_up, pass_on = event

        def run():
            if slot == "relay":
                remote(
                    relay_piece(piece), relay_piece(piece),
                    relay_send.at[piece], relay_recv.at[piece], (above, y),
                ).wait_recv()
                send_relay(piece, column).start()
                return
            remote(
                slot_piece(slot, core, piece), slot_piece(slot, core, piece),
                pair_send.at[slot, piece], slot_recv.at[slot, piece], (pair, y),
            ).wait_recv()
            if to_right:
                forward(slot, piece, True).start()
            if to_left:
                forward(slot, piece, False).start()
            if pass_on == "both" or pass_on == "own":
                hand_over(slot, piece).start()
            if pass_on == "own_wait":

                @pl.when(core == 1)
                def _():
                    hand_over(slot, piece).start()

        if pass_on == "own":
            pl.when(core == 1)(run)
        else:
            run()

    schedules = [arrivals(column) for column in range(COLUMNS)]

    def prefixes(until):
        for column in range(COLUMNS):
            due = [event for event in schedules[column] if event[0] <= until]
            if not due:
                continue
            schedules[column] = schedules[column][len(due) :]

            @pl.when(x == column)
            def _():
                for event in due:
                    handle(column, event)

    def project(hop):
        start = pl.multiple_of(block_at(hop) * 512, 512)
        rows = pl.ds(start, 512)
        for copy in weight_copies(hop):
            copy.wait()
        block = xbuf[block_at(hop)]
        for weight, first, size in ((wq, 0, 512), (wk, 512, 128), (wv, 640, 128)):
            part = jnp.dot(block, weight[rows, :], preferred_element_type=jnp.float32)
            if hop == 0:
                acc[:, first : first + size] = part
            else:
                acc[:, first : first + size] += part

    own_x.wait()
    project(0)
    times = {(0, 0): 4.2, (0, 1): 5.6, (1, 0): 7.3, (1, 1): 8.7, (2, 0): 10.4, (2, 1): 11.8}
    for hop in range(3):
        for half in range(2):
            for way in range(2):
                x_arrival(way, hop, half).wait_recv()
                if x_sent(way, hop + 1, half):
                    x_copy(way, hop + 1, half).start()
            prefixes(times[hop, half])
        project(-(hop + 1))
        project(hop + 1)
    prefixes(12.5)
    for way in range(2):
        x_arrival(way, 3, way).wait_recv()
    project(4)
    prefixes(99.0)
    for group in range(4):
        q_ref[group * 128 : (group + 1) * 128, :] = acc[:, group * 128 : (group + 1) * 128].astype(jnp.bfloat16)
    k_ref[...] = acc[:, 512:640].astype(jnp.bfloat16)
    v_ref[...] = acc[:, 640:768].astype(jnp.bfloat16)

    own_k.wait()
    own_v.wait()
    for slot in range(COLUMNS):
        for piece in range(4):
            remote(
                slot_piece(slot, 1 - core, piece), slot_piece(slot, 1 - core, piece),
                pair_send.at[slot, piece], pair_recv.at[slot, piece], (pair, y),
            ).wait_recv()

    for hop in range(4):
        for half in range(2):
            for way in range(2):
                if x_sent(way, hop, half):
                    x_copy(way, hop, half).wait_send()
    for column in range(COLUMNS):

        @pl.when(x == column)
        def _():
            for piece in range(4):
                send_left(piece, column).wait_send()
                if column < 3:
                    send_right(piece).wait_send()
                    send_relay(piece, column).wait_send()
                else:
                    send_up(piece).wait_send()
            for _, slot, piece, to_right, to_left, _, pass_on in arrivals(column):
                if to_right:
                    forward(slot, piece, True).wait_send()
                if to_left:
                    forward(slot, piece, False).wait_send()
                if pass_on == "both":
                    hand_over(slot, piece).wait_send()

    @pl.when((core == 1) & (x < 3))
    def _():
        for piece in range(4):
            send_up(piece).wait_send()

    for piece in range(4):
        hand_own(piece).wait_send()


def gather(slice_rows, w_query, w_key, w_value, prefix_keys, prefix_values):
    bf16, f32 = jnp.bfloat16, jnp.float32
    dma = pltpu.SemaphoreType.DMA
    anywhere = pl.BlockSpec(memory_space=pl.ANY)
    vmem = pl.BlockSpec(memory_space=pltpu.VMEM)
    return pl.pallas_call(
        gather_kernel,
        out_shape=(
            pltpu.VMEM((512, HEAD_DIM), bf16),
            pltpu.VMEM((128, HEAD_DIM), bf16),
            pltpu.VMEM((128, HEAD_DIM), bf16),
            pltpu.VMEM((9, 2, 512, HEAD_DIM), bf16),
        ),
        in_specs=[anywhere] * 6,
        out_specs=(vmem,) * 4,
        scratch_shapes=[
            pltpu.VMEM((RING, 128, 512), bf16),
            pltpu.VMEM((4096, 512), bf16),
            pltpu.VMEM((4096, 128), bf16),
            pltpu.VMEM((4096, 128), bf16),
            pltpu.VMEM((128, 768), f32),
            pltpu.VMEM((2, 512, HEAD_DIM), bf16),
            dma((8, 3)), dma((3,)), dma((2, 8)), dma((2, 8)),
            dma((4,)), dma((4,)), dma((4,)), dma((4,)), dma((4,)), dma((4,)), dma((4, 4)),
            dma((4, 4)), dma((4,)), dma((4, 4)),
        ],
        compiler_params=pltpu.CompilerParams(
            collective_id=0, has_side_effects=True, vmem_limit_bytes=32 * 1024 * 1024
        ),
        name="gather",
    )(slice_rows, w_query, w_key, w_value, prefix_keys, prefix_values)


def scores_of(keys, queries):
    return lax.dot_general(
        keys, queries, (((1,), (1,)), ((), ())), preferred_element_type=jnp.float32
    )


def weigh(values, weights):
    return lax.dot_general(
        values, weights, (((0,), (0,)), ((), ())), preferred_element_type=jnp.float32
    )


def attend_kernel(pb_ref, q_ref, k_ref, v_ref, kv_ref, out_ref, scores, m_ref, l_ref, o_ref):
    section = lax.axis_index("section")
    factor = math.log2(math.e) / math.sqrt(HEAD_DIM)
    never = 1e30
    queries = q_ref[...]

    def slot_of(offset):
        return 8 if offset == 0 else lax.rem(section - offset + 64, 8)

    key_row = lax.broadcasted_iota(jnp.int32, (128, 512), 0)
    query_row = lax.broadcasted_iota(jnp.int32, (128, 512), 1) % 128
    own = jnp.where(key_row <= query_row, scores_of(k_ref[...], queries), -never)
    top = jnp.max(own, axis=0, keepdims=True)
    for offset in range(REACH + 1):
        part = scores_of(kv_ref[slot_of(offset), 0, :BLOCK, :], queries)
        scores[offset] = part
        peak = jnp.max(part, axis=0, keepdims=True)
        top = jnp.maximum(top, jnp.where(section >= offset, peak, -never))
    weights = jnp.exp2((own - top) * factor)
    total = jnp.sum(weights, axis=0, keepdims=True)
    result = weigh(v_ref[...], weights.astype(jnp.bfloat16))
    for offset in range(REACH + 1):
        shift = jnp.where(section >= offset, top, never)
        weights = jnp.exp2((scores[offset] - shift) * factor)
        total += jnp.sum(weights, axis=0, keepdims=True)
        result += weigh(kv_ref[slot_of(offset), 1, :BLOCK, :], weights.astype(jnp.bfloat16))
    m_ref[...] = top
    l_ref[...] = total
    o_ref[...] = result

    for offset in range(REACH + 1):
        blocks = pb_ref[jnp.maximum(section - offset, 0)]

        @pl.when((section >= offset) & (blocks > 1))
        def _():
            part = scores_of(kv_ref[slot_of(offset), 0, BLOCK:, :], queries)
            before = m_ref[...]
            after = jnp.maximum(before, jnp.max(part, axis=0, keepdims=True))
            keep = jnp.exp2((before - after) * factor)
            weights = jnp.exp2((part - after) * factor)
            m_ref[...] = after
            l_ref[...] = l_ref[...] * keep + jnp.sum(weights, axis=0, keepdims=True)
            o_ref[...] = o_ref[...] * keep + weigh(
                kv_ref[slot_of(offset), 1, BLOCK:, :], weights.astype(jnp.bfloat16)
            )

    final = o_ref[...] / l_ref[...]
    for group in range(4):
        part = final[:, group * 128 : (group + 1) * 128]
        out_ref[:, group * 128 : (group + 1) * 128] = part.T.astype(jnp.bfloat16)


def attend(prefix_blocks, queries, own_keys, own_values, kv):
    vmem = pl.BlockSpec(memory_space=pltpu.VMEM)
    return pl.pallas_call(
        attend_kernel,
        out_shape=jax.ShapeDtypeStruct((128, 512), jnp.bfloat16),
        in_specs=[pl.BlockSpec(memory_space=pltpu.SMEM)] + [vmem] * 4,
        out_specs=vmem,
        scratch_shapes=[
            pltpu.VMEM((REACH + 1, BLOCK, 512), jnp.float32),
            pltpu.VMEM((1, 512), jnp.float32),
            pltpu.VMEM((1, 512), jnp.float32),
            pltpu.VMEM((HEAD_DIM, 512), jnp.float32),
        ],
        compiler_params=pltpu.CompilerParams(vmem_limit_bytes=24 * 1024 * 1024),
        name="attend",
    )(prefix_blocks, queries, own_keys, own_values, kv)


def on_device(slice_rows, w_query, w_key, w_value, prefix_keys, prefix_values, prefix_blocks):
    queries, own_keys, own_values, kv = gather(
        slice_rows, w_query, w_key, w_value, prefix_keys, prefix_values
    )
    return attend(prefix_blocks, queries, own_keys, own_values, kv)


def solution(mesh):
    in_specs = (
        P("section", "head"),
        P(None, "head"),
        P(None, "head"),
        P(None, "head"),
        P("section", "head"),
        P("section", "head"),
        P(),
    )
    out_specs = P("section", "head")
    return jax.shard_map(
        on_device, mesh=mesh, in_specs=in_specs, out_specs=out_specs, check_vma=False
    )
```

time: 111 us -> 45.4 us (0.41)
  the two profiles are of different devices: /device:TPU:207 before, /device:TPU:17 now
where the time goes in v1:
time: 45.4 us; the launch traced here: 44.8 us
  Pallas kernels  37.5 us (83%)
  local copies, waits for them, and re-layouts  7.35 us (16%)
    pallas_call x1, Pallas kernels, gather(): pl.pallas_call(gather_kernel, out_shape=(pltpu.VMEM((512, HEAD_DIM), bf16...  34.1 us
    unnamed x14, local copies, waits for them, and re-layouts  7.35 us
    pallas_call x1, Pallas kernels, attend(): pl.pallas_call(attend_kernel, out_shape=jax.ShapeDtypeStruct((128, 512),...  3.34 us

profile of v1, /device:TPU:17, one launch (start us, length us, event | category | flops | bytes accessed | tf_op | source)
XLA Modules:
  0.0 44.8 jit_solution(15244671802150067577)
XLA Ops:
  0.0 0.0 copy-start
  0.0 2.2 %copy-done = bf16[4096,512]{1,0:T(8,128)(2,1)S(1)} copy-done((bf16[4096,512]{1,0:T(8,128)(2,1)S(1)}, bf16[4096,512]{1,0:T(8,128)(2,1)}, u32[]{:S(2)}) %copy-start) | copy-done | bytes 4194328
  2.2 0.0 copy-start.1
  2.2 1.2 %copy-done.1 = bf16[4096,128]{1,0:T(8,128)(2,1)S(1)} copy-done((bf16[4096,128]{1,0:T(8,128)(2,1)S(1)}, bf16[4096,128]{1,0:T(8,128)(2,1)}, u32[]{:S(2)}) %copy-start.1) | copy-done | bytes 1048600
  3.4 0.0 copy-start.2
  3.4 1.2 %copy-done.2 = bf16[4096,128]{1,0:T(8,128)(2,1)S(1)} copy-done((bf16[4096,128]{1,0:T(8,128)(2,1)S(1)}, bf16[4096,128]{1,0:T(8,128)(2,1)}, u32[]{:S(2)}) %copy-start.2) | copy-done | bytes 1048600
  4.6 0.0 copy-start.3
  4.6 0.9 %copy-done.3 = bf16[128,512]{1,0:T(8,128)(2,1)S(1)} copy-done((bf16[128,512]{1,0:T(8,128)(2,1)S(1)}, bf16[128,512]{1,0:T(8,128)(2,1)}, u32[]{:S(2)}) %copy-start.3) | copy-done | bytes 131096
  5.5 0.0 copy-start.4
  5.5 0.9 %copy-done.4 = bf16[512,128]{1,0:T(8,128)(2,1)S(1)} copy-done((bf16[512,128]{1,0:T(8,128)(2,1)S(1)}, bf16[512,128]{1,0:T(8,128)(2,1)}, u32[]{:S(2)}) %copy-start.4) | copy-done | bytes 131096
  6.4 0.0 copy-start.5
  6.5 0.9 %copy-done.5 = bf16[512,128]{1,0:T(8,128)(2,1)S(1)} copy-done((bf16[512,128]{1,0:T(8,128)(2,1)S(1)}, bf16[512,128]{1,0:T(8,128)(2,1)}, u32[]{:S(2)}) %copy-start.5) | copy-done | bytes 131096
  7.4 0.0 copy-start.6
  7.4 34.1 %gather.1 = (bf16[512,128]{1,0:T(8,128)(2,1)S(1)}, bf16[128,128]{1,0:T(8,128)(2,1)S(1)}, bf16[128,128]{1,0:T(8,128)(2,1)S(1)}, bf16[9,2,512,128]{3,2,1,0:T(8,128)(2,1)S(1)}) custom-call(bf16[128,512]{1,0:T(8,128)(2,1)S(1)} %copy-done.3, bf16[4096,512]{1,0:T(8,128)(2,1)S(1)} %copy-done, bf16[4096,128]{1,0:T(8,128)(2,1)S(1)} %copy-done.1, ...), custom_call_target="tpu_custom_call" | custom-call | tf_op jit(solution)/shard_map/gather/pallas_call | solution.py:365
  41.5 0.0 copy-done.6
  41.5 3.3 %attend.1 = bf16[128,512]{1,0:T(8,128)(2,1)} custom-call(s32[64]{0:T(128)S(1)} %copy-done.6, bf16[512,128]{1,0:T(8,128)(2,1)S(1)} %get-tuple-element.9.q_ref, bf16[128,128]{1,0:T(8,128)(2,1)S(1)} %get-tuple-element.10.k_ref, bf16[128,128]{1,0:T(8,128)(2,1)S(1)} %get-tuple-element.11.v_ref, bf16[9,2,512,128]{3,2,1,0:T(8,128)(2,1)S(1)} %get-tuple-element.12.kv_ref), custom_call_target="tpu_custom_call" | custom-call | tf_op jit(solution)/shard_map/attend/pallas_call | solution.py:459
Async XLA Ops:
  0.0 2.2 %copy-start = (bf16[4096,512]{1,0:T(8,128)(2,1)S(1)}, bf16[4096,512]{1,0:T(8,128)(2,1)}, u32[]{:S(2)}) copy-start(bf16[4096,512]{1,0:T(8,128)(2,1)} %wq_ref.1) | copy-start | bytes 12582916
  2.2 1.2 %copy-start.1 = (bf16[4096,128]{1,0:T(8,128)(2,1)S(1)}, bf16[4096,128]{1,0:T(8,128)(2,1)}, u32[]{:S(2)}) copy-start(bf16[4096,128]{1,0:T(8,128)(2,1)} %wk_ref.1) | copy-start | bytes 3145732
  3.4 1.2 %copy-start.2 = (bf16[4096,128]{1,0:T(8,128)(2,1)S(1)}, bf16[4096,128]{1,0:T(8,128)(2,1)}, u32[]{:S(2)}) copy-start(bf16[4096,128]{1,0:T(8,128)(2,1)} %wv_ref.1) | copy-start | bytes 3145732
  4.6 0.9 %copy-start.3 = (bf16[128,512]{1,0:T(8,128)(2,1)S(1)}, bf16[128,512]{1,0:T(8,128)(2,1)}, u32[]{:S(2)}) copy-start(bf16[128,512]{1,0:T(8,128)(2,1)} %x_ref.1) | copy-start | bytes 393220
  5.5 0.9 %copy-start.4 = (bf16[512,128]{1,0:T(8,128)(2,1)S(1)}, bf16[512,128]{1,0:T(8,128)(2,1)}, u32[]{:S(2)}) copy-start(bf16[512,128]{1,0:T(8,128)(2,1)} %pk_ref.1) | copy-start | bytes 393220
  6.4 0.9 %copy-start.5 = (bf16[512,128]{1,0:T(8,128)(2,1)S(1)}, bf16[512,128]{1,0:T(8,128)(2,1)}, u32[]{:S(2)}) copy-start(bf16[512,128]{1,0:T(8,128)(2,1)} %pv_ref.1) | copy-start | bytes 393220
  7.4 34.1 %copy-start.6 = (s32[64]{0:T(128)S(1)}, s32[64]{0:T(128)}, u32[]{:S(2)}) copy-start(s32[64]{0:T(128)} %pb_ref.1) | copy-start | bytes 772

commit v2 on v0

v2 whole, which is shorter than its diff:
```python
import functools
import math

import jax
import jax.numpy as jnp
from jax import lax
from jax.experimental import pallas as pl
from jax.experimental.pallas import tpu as pltpu
from jax.sharding import PartitionSpec as P

HEAD_DIM = 128
BLOCK = 256
REACH = 7
COLUMNS = 4
LAYERS = 8
RING = 8
MESH = pl.DeviceIdType.MESH

LOW_FIRST = [0, 1, 2, 3]
HIGH_FIRST = [2, 3, 0, 1]
LOW, HIGH = (0, 1), (2, 3)
PIECES = 4
PIECE = 128 // PIECES


def rows_of(piece):
    return pl.ds((piece // 2) * BLOCK, BLOCK)


def steps(first, each=1.4):
    return [first + each * index for index in range(4)]


def arrivals(column):
    events = []

    def add(times, slot, order=LOW_FIRST, kinds=(0, 1), right=(), left=(), up=False, pair=True):
        for kind in kinds:
            for time, piece in zip(times, order):
                events.append(
                    dict(
                        time=time + 0.3 * kind, slot=slot, kind=kind, piece=piece,
                        right=piece in right, left=piece in left, up=up, pair=pair,
                        prev=slot != "relay" and slot >= column,
                    )
                )

    every = LOW + HIGH
    direct, relayed = steps(4.2), steps(6.6)
    if column < 3:
        add(steps(4.0, 0.7), column, kinds=(1,))
        add(direct, "relay", HIGH_FIRST if column == 2 else LOW_FIRST, up=True, pair=False)
    if column == 0:
        add(relayed, 1)
        add(steps(7.4), 3, right=LOW)
        add(steps(9.0), 2)
    elif column == 1:
        add(direct, 0, right=LOW)
        add(relayed, 2, left=every)
        add([9.8, 11.2], 3, LOW)
        add([9.0, 10.4], 3, HIGH)
    elif column == 2:
        add(direct, 1, right=every)
        add(relayed, 3, HIGH_FIRST, left=HIGH)
        add([8.0, 9.4], 0, LOW)
        add([8.0, 9.4], 0, HIGH)
    else:
        add(steps(4.8), 3, kinds=(0,), right=every, pair=False)
        add(steps(4.8), 3, kinds=(1,), right=every)
        add(direct, 2)
        add(direct, 0, HIGH_FIRST, left=HIGH)
        add(steps(8.0), 1)
    return sorted(events, key=lambda event: event["time"])


def gather_kernel(
    x_ref, wq_ref, wk_ref, wv_ref, pk_ref, pv_ref,
    q_ref, k_ref, v_ref, kv_ref,
    xbuf, xother, wq, wk, wv, acc, relay,
    w_sem, local_sem, x_send, x_recv, x_pair_send, x_pair_recv,
    right_send, left_send, up_send, own_send, relay_send, right_fwd, left_fwd, pair_send,
    slot_recv, relay_recv, pair_recv, ready,
):
    section = lax.axis_index("section")
    y = lax.axis_index("head")
    core = lax.rem(section, 2)
    x = lax.rem(lax.div(section, 2), COLUMNS)
    z = lax.div(section, 2 * COLUMNS)

    def at(layer, column, kind, ring=None):
        return ((layer * COLUMNS + column) * 2 + kind, y if ring is None else ring)

    x_right, x_left = lax.rem(x + 1, COLUMNS), lax.rem(x + COLUMNS - 1, COLUMNS)
    z_above, z_below = lax.rem(z + 1, LAYERS), lax.rem(z + LAYERS - 1, LAYERS)
    y_up, y_down = lax.rem(y + 1, RING), lax.rem(y + RING - 1, RING)
    right, left = at(z, x_right, 1), at(z, x_left, 1)
    above = at(z_above, x, 1)
    ways = (at(z, x, 1, y_up), at(z, x, 1, y_down))
    pair = at(z, x, 1 - core)

    def block_at(hop):
        return lax.rem(y + hop + RING, RING)

    visits = [0, -1, 1, -2, 2, -3, 3, 4]

    def weight_copies(hop):
        start = pl.multiple_of(block_at(hop) * 512, 512)
        rows = pl.ds(start, 512)
        place = visits.index(hop)
        return [
            pltpu.make_async_copy(source.at[rows], target.at[rows], w_sem.at[place, index])
            for index, (source, target) in enumerate(((wq_ref, wq), (wk_ref, wk), (wv_ref, wv)))
        ]

    def project(hop):
        start = pl.multiple_of(block_at(hop) * 512, 512)
        rows = pl.ds(start, 512)
        for copy in weight_copies(hop):
            copy.wait()
        block = xbuf[block_at(hop)]
        for weight, first, size in ((wq, 0, 512), (wk, 512, 128), (wv, 640, 128)):
            part = jnp.dot(block, weight[rows, :], preferred_element_type=jnp.float32)
            if hop == 0:
                acc[:, first : first + size] = part
            else:
                acc[:, first : first + size] += part

    def remote(source, target, send, recv, device):
        return pltpu.make_async_remote_copy(
            src_ref=source, dst_ref=target, send_sem=send, recv_sem=recv,
            device_id=device, device_id_type=MESH,
        )

    own_x = pltpu.make_async_copy(x_ref, xbuf.at[y], local_sem.at[0])
    own_k = pltpu.make_async_copy(pk_ref, kv_ref.at[8, 0], local_sem.at[1])
    own_v = pltpu.make_async_copy(pv_ref, kv_ref.at[8, 1], local_sem.at[2])
    own_x.start()
    for copy in weight_copies(0):
        copy.start()

    def tell(semaphore, device):
        pl.semaphore_signal(semaphore, inc=1, device_id=device, device_id_type=MESH)

    barrier = pltpu.get_barrier_semaphore()

    @pl.when(core == 1)
    def _():
        for kind in range(2):
            for device in (
                at(z, x, kind, y_up), at(z, x, kind, y_down),
                at(z, x_right, kind), at(z, x_left, kind),
            ):
                tell(barrier, device)

    tell(barrier, pair)

    @pl.when((z < LAYERS - 1) & ((core == 1) | (x == 3)))
    def _():
        tell(barrier, above)

    for hop in visits[1:]:
        for copy in weight_copies(hop):
            copy.start()
    own_k.start()
    own_v.start()
    below_count = jnp.where((core == 1) & (z > 0), jnp.where(x == 3, 2, 1), 0)
    pl.semaphore_wait(barrier, 5 + below_count)

    @pl.when((core == 1) & (z > 0))
    def _():
        tell(ready, at(z_below, x, 1))

        @pl.when(x == 3)
        def _():
            tell(ready, at(z_below, x, 0))

    def rows_at(piece):
        return pl.ds(piece * PIECE, PIECE)

    def x_own(way, piece, kind):
        target = xother if kind == 0 else xbuf
        return remote(
            x_ref.at[rows_at(piece)], target.at[y, rows_at(piece)],
            x_send.at[way, kind, piece], x_recv.at[way, kind, piece], ways[way],
        )

    def x_origin(way, hop):
        return block_at(-hop - 1 if way == 0 else hop + 1)

    def x_piece(way, hop, piece, kind):
        return (xother if kind == 0 else xbuf).at[x_origin(way, hop), rows_at(piece)]

    def x_arrival(way, hop, piece, kind):
        here = x_piece(way, hop, piece, kind)
        index = hop * PIECES + piece
        return remote(here, here, x_send.at[way, kind, index], x_recv.at[way, kind, index], ways[way])

    def x_forward(way, hop, piece, kind):
        here = x_piece(way, hop, piece, kind)
        index = (hop + 1) * PIECES + piece
        return remote(here, here, x_send.at[way, kind, index], x_recv.at[way, kind, index], ways[way])

    def x_hand(way, hop, piece):
        index = hop * PIECES + piece
        rows = rows_at(piece)
        return remote(
            xother.at[x_origin(way, hop), rows], xbuf.at[x_origin(way, hop), rows],
            x_pair_send.at[way, index], x_pair_recv.at[way, index], pair,
        )

    def travels(way, hop, piece):
        return hop < 3 or (hop == 3 and piece // (PIECES // 2) == way)

    def own_piece(piece):
        return (pk_ref if piece % 2 == 0 else pv_ref).at[rows_of(piece)]

    def slot_piece(column, kind, piece):
        return kv_ref.at[column * 2 + kind, piece % 2, rows_of(piece)]

    def relay_piece(kind, piece):
        return relay.at[kind, piece % 2, rows_of(piece)]

    def send_right(kind, piece, column):
        return remote(
            own_piece(piece), slot_piece(column, kind, piece),
            right_send.at[piece], slot_recv.at[column * 2 + kind, piece], right,
        )

    def send_left(kind, piece, column):
        if column == 0:
            target, arrived = slot_piece(0, kind, piece), slot_recv.at[kind, piece]
        else:
            target, arrived = relay_piece(kind, piece), relay_recv.at[kind, piece]
        return remote(own_piece(piece), target, left_send.at[piece], arrived, left)

    def send_up(kind, piece):
        if kind == 0:
            target, arrived = relay_piece(0, piece), relay_recv.at[0, piece]
        else:
            target, arrived = slot_piece(x, 1, piece), slot_recv.at[x * 2 + 1, piece]
        return remote(own_piece(piece), target, up_send.at[piece], arrived, above)

    def send_pair(piece):
        return remote(
            own_piece(piece), slot_piece(x, 0, piece),
            own_send.at[piece], pair_recv.at[x * 2, piece], pair,
        )

    def first_sends(kind, column):
        order = HIGH_FIRST if column in (0, 3) else LOW_FIRST
        for index in range(4):
            piece = order[index]
            yield column > 0, functools.partial(send_left, kind, piece, column)
            if column < 3:
                yield False, functools.partial(send_right, kind, index, column)

    def source_of(event, column):
        kind, piece = event["kind"], event["piece"]
        if event["slot"] == "relay" or (column == 3 and event["slot"] == 3 and kind == 0):
            return relay_piece(kind, piece), relay_recv.at[kind, piece]
        slot = event["slot"]
        return slot_piece(slot, kind, piece), slot_recv.at[slot * 2 + kind, piece]

    def sends_of(event, column):
        kind, piece, slot = event["kind"], event["piece"], event["slot"]
        source, _ = source_of(event, column)
        copies = []
        if event["up"]:
            return [
                remote(
                    source, slot_piece(column + 1, kind, piece), relay_send.at[kind, piece],
                    slot_recv.at[(column + 1) * 2 + kind, piece], above,
                )
            ]
        target, arrived = slot_piece(slot, kind, piece), slot_recv.at[slot * 2 + kind, piece]
        if event["right"]:
            copies.append(remote(source, target, right_fwd.at[kind, piece], arrived, right))
        if event["left"]:
            copies.append(remote(source, target, left_fwd.at[kind, piece], arrived, left))
        if event["pair"]:
            copies.append(
                remote(
                    source, target, pair_send.at[slot * 2 + kind, piece],
                    pair_recv.at[slot * 2 + kind, piece], pair,
                )
            )
        return copies

    def guarded(condition, run):
        if condition is None:
            run()
        else:
            pl.when(condition)(run)

    def start_first(kind):
        for piece in range(PIECES):
            for way in range(2):
                x_own(way, piece, kind).start()
        for column in range(COLUMNS):

            @pl.when(x == column)
            def _():
                plain = [make for needs, make in first_sends(kind, column) if not needs]
                needing = [make for needs, make in first_sends(kind, column) if needs]
                if needing:

                    @pl.when(z < LAYERS - 1)
                    def _():
                        for make in needing:
                            make().start()

                for make in plain:
                    make().start()

    def finish_first(kind):
        for piece in range(PIECES):
            for way in range(2):
                x_own(way, piece, kind).wait_send()
        for column in range(COLUMNS):

            @pl.when(x == column)
            def _():
                for needs, make in first_sends(kind, column):
                    if not needs:
                        make().wait_send()
                if column > 0:

                    @pl.when(z < LAYERS - 1)
                    def _():
                        for needs, make in first_sends(kind, column):
                            if needs:
                                make().wait_send()

    @pl.when(z == 0)
    def _():
        for column in range(COLUMNS):

            @pl.when(x == column)
            def _():
                for slot in range(column * 2 + 2, COLUMNS * 2):
                    kv_ref[slot] = jnp.zeros((2, 512, HEAD_DIM), jnp.bfloat16)

                @pl.when(core == 0)
                def _():
                    kv_ref[column * 2 + 1] = jnp.zeros((2, 512, HEAD_DIM), jnp.bfloat16)

    @pl.when(core == 0)
    def _():
        start_first(0)
        for piece in range(4):
            send_pair(piece).start()
        own_x.wait()
        project(0)

        @pl.when((x == 3) & (z < LAYERS - 1))
        def _():
            pl.semaphore_wait(ready, 1)
            for piece in range(4):
                send_up(0, piece).start()

        for hop in range(4):
            for way in range(2):
                for piece in range(PIECES):
                    if travels(way, hop, piece):
                        x_hand(way, hop, piece).wait_recv()
                if hop < 3:
                    project(-hop - 1 if way == 0 else hop + 1)
        project(4)
        for column in range(COLUMNS):

            @pl.when(x == column)
            def _():
                def take(slot, kind):
                    for piece in range(4):
                        here = slot_piece(slot, kind, piece)
                        index = slot * 2 + kind
                        remote(
                            here, here, pair_send.at[index, piece], pair_recv.at[index, piece], pair
                        ).wait_recv()

                for slot in range(column):
                    for kind in range(2):
                        take(slot, kind)

                @pl.when(z > 0)
                def _():
                    take(column, 1)
                    for slot in range(column + 1, COLUMNS):
                        for kind in range(2):
                            take(slot, kind)

        finish_first(0)
        for piece in range(4):
            send_pair(piece).wait_send()

        @pl.when((x == 3) & (z < LAYERS - 1))
        def _():
            for piece in range(4):
                send_up(0, piece).wait_send()

    schedules = [arrivals(column) for column in range(COLUMNS)]

    def handle(event, column):
        source, arrived = source_of(event, column)

        def run():
            remote(source, source, pair_send.at[0, 0], arrived, pair).wait_recv()
            if event["up"]:

                @pl.when(z > 0)
                def _():
                    for copy in sends_of(event, column):
                        copy.start()

            else:
                for copy in sends_of(event, column):
                    copy.start()

        guarded(condition_of(event), run)

    def condition_of(event):
        return z < LAYERS - 1 if event["up"] else z > 0 if event["prev"] else None

    def prefixes(until):
        for column in range(COLUMNS):
            due = [event for event in schedules[column] if event["time"] <= until]
            if not due:
                continue
            schedules[column] = schedules[column][len(due) :]

            @pl.when(x == column)
            def _():
                for event in due:
                    handle(event, column)

    def lowest_goes_up():
        @pl.when(z == 0)
        def _():
            pl.semaphore_wait(ready, 1)
            for piece in range(4):
                send_up(1, piece).start()
            for column in range(COLUMNS - 1):

                @pl.when(x == column)
                def _():
                    for event in arrivals(column):
                        if event["up"]:
                            for copy in sends_of(event, column):
                                copy.start()

    @pl.when(core == 1)
    def _():
        start_first(1)

        @pl.when((z > 0) & (z < LAYERS - 1))
        def _():
            pl.semaphore_wait(ready, 1)
            for piece in range(4):
                send_up(1, piece).start()

        own_x.wait()
        project(0)
        clock = {0: 3.5, 1: 5.9, 2: 8.3, 3: 10.7}
        for hop in range(4):
            for piece in range(PIECES):
                if hop == 3 and piece >= PIECES // 2:
                    continue
                for kind in range(2):
                    for way in range(2):
                        this = piece if hop < 3 or way == 0 else piece + PIECES // 2
                        x_arrival(way, hop, this, kind).wait_recv()
                        if travels(way, hop + 1, this):
                            x_forward(way, hop, this, kind).start()
                        if kind == 0:
                            x_hand(way, hop, this).start()
                prefixes(clock[hop] + 2.4 / PIECES * piece)
                if hop > 0 and piece == 0:
                    project(-hop)
                if hop > 0 and piece == 1:
                    project(hop)
                if hop == 2 and piece == 1:
                    lowest_goes_up()
        project(4)
        prefixes(99.0)
        for piece in range(4):
            here = slot_piece(x, 0, piece)
            remote(here, here, pair_send.at[0, 0], pair_recv.at[x * 2, piece], pair).wait_recv()

        finish_first(1)
        for hop in range(4):
            for piece in range(PIECES):
                for way in range(2):
                    for kind in range(2):
                        if travels(way, hop + 1, piece):
                            x_forward(way, hop, piece, kind).wait_send()
                    if travels(way, hop, piece):
                        x_hand(way, hop, piece).wait_send()

        @pl.when(z < LAYERS - 1)
        def _():
            for piece in range(4):
                send_up(1, piece).wait_send()

        for column in range(COLUMNS):

            @pl.when(x == column)
            def _():
                events = arrivals(column)
                for event in events:
                    if not event["up"] and not event["prev"]:
                        for copy in sends_of(event, column):
                            copy.wait_send()

                @pl.when(z > 0)
                def _():
                    for event in events:
                        if event["prev"]:
                            for copy in sends_of(event, column):
                                copy.wait_send()

                @pl.when(z < LAYERS - 1)
                def _():
                    for event in events:
                        if event["up"]:
                            for copy in sends_of(event, column):
                                copy.wait_send()

    for group in range(4):
        q_ref[group * 128 : (group + 1) * 128, :] = acc[:, group * 128 : (group + 1) * 128].astype(jnp.bfloat16)
    k_ref[...] = acc[:, 512:640].astype(jnp.bfloat16)
    v_ref[...] = acc[:, 640:768].astype(jnp.bfloat16)
    own_k.wait()
    own_v.wait()


def gather(slice_rows, w_query, w_key, w_value, prefix_keys, prefix_values):
    bf16, f32 = jnp.bfloat16, jnp.float32
    dma = pltpu.SemaphoreType.DMA
    anywhere = pl.BlockSpec(memory_space=pltpu.HBM)
    vmem = pl.BlockSpec(memory_space=pltpu.VMEM)
    return pl.pallas_call(
        gather_kernel,
        out_shape=(
            pltpu.VMEM((512, HEAD_DIM), bf16),
            pltpu.VMEM((128, HEAD_DIM), bf16),
            pltpu.VMEM((128, HEAD_DIM), bf16),
            pltpu.VMEM((9, 2, 512, HEAD_DIM), bf16),
        ),
        in_specs=[anywhere] * 6,
        out_specs=(vmem,) * 4,
        scratch_shapes=[
            pltpu.VMEM((RING, 128, 512), bf16),
            pltpu.VMEM((RING, 128, 512), bf16),
            pltpu.VMEM((4096, 512), bf16),
            pltpu.VMEM((4096, 128), bf16),
            pltpu.VMEM((4096, 128), bf16),
            pltpu.VMEM((128, 768), f32),
            pltpu.VMEM((2, 2, 512, HEAD_DIM), bf16),
            dma((8, 3)), dma((3,)),
            dma((2, 2, 4 * PIECES)), dma((2, 2, 4 * PIECES)), dma((2, 4 * PIECES)), dma((2, 4 * PIECES)),
            dma((4,)), dma((4,)), dma((4,)), dma((4,)),
            dma((2, 4)), dma((2, 4)), dma((2, 4)), dma((8, 4)),
            dma((8, 4)), dma((2, 4)), dma((8, 4)), pltpu.SemaphoreType.REGULAR,
        ],
        compiler_params=pltpu.CompilerParams(
            collective_id=0, has_side_effects=True, vmem_limit_bytes=58 * 1024 * 1024
        ),
        name="gather",
    )(slice_rows, w_query, w_key, w_value, prefix_keys, prefix_values)


def scores_of(keys, queries):
    return lax.dot_general(
        keys, queries, (((1,), (1,)), ((), ())), preferred_element_type=jnp.float32
    )


def weigh(values, weights):
    return lax.dot_general(
        values, weights, (((0,), (0,)), ((), ())), preferred_element_type=jnp.float32
    )


def attend_kernel(pb_ref, q_ref, k_ref, v_ref, kv_ref, out_ref, scores, m_ref, l_ref, o_ref):
    section = lax.axis_index("section")
    factor = math.log2(math.e) / math.sqrt(HEAD_DIM)
    never = 1e30
    queries = q_ref[...]

    def slot_of(offset):
        return 8 if offset == 0 else lax.rem(section - offset + 64, 8)

    key_row = lax.broadcasted_iota(jnp.int32, (128, 512), 0)
    query_row = lax.broadcasted_iota(jnp.int32, (128, 512), 1) % 128
    own = jnp.where(key_row <= query_row, scores_of(k_ref[...], queries), -never)
    top = jnp.max(own, axis=0, keepdims=True)
    for offset in range(REACH + 1):
        part = scores_of(kv_ref[slot_of(offset), 0, :BLOCK, :], queries)
        scores[offset] = part
        peak = jnp.max(part, axis=0, keepdims=True)
        top = jnp.maximum(top, jnp.where(section >= offset, peak, -never))
    weights = jnp.exp2((own - top) * factor)
    total = jnp.sum(weights, axis=0, keepdims=True)
    result = weigh(v_ref[...], weights.astype(jnp.bfloat16))
    for offset in range(REACH + 1):
        shift = jnp.where(section >= offset, top, never)
        weights = jnp.exp2((scores[offset] - shift) * factor)
        total += jnp.sum(weights, axis=0, keepdims=True)
        result += weigh(kv_ref[slot_of(offset), 1, :BLOCK, :], weights.astype(jnp.bfloat16))
    m_ref[...] = top
    l_ref[...] = total
    o_ref[...] = result

    for offset in range(REACH + 1):
        blocks = pb_ref[jnp.maximum(section - offset, 0)]

        @pl.when((section >= offset) & (blocks > 1))
        def _():
            part = scores_of(kv_ref[slot_of(offset), 0, BLOCK:, :], queries)
            before = m_ref[...]
            after = jnp.maximum(before, jnp.max(part, axis=0, keepdims=True))
            keep = jnp.exp2((before - after) * factor)
            weights = jnp.exp2((part - after) * factor)
            m_ref[...] = after
            l_ref[...] = l_ref[...] * keep + jnp.sum(weights, axis=0, keepdims=True)
            o_ref[...] = o_ref[...] * keep + weigh(
                kv_ref[slot_of(offset), 1, BLOCK:, :], weights.astype(jnp.bfloat16)
            )

    final = o_ref[...] / l_ref[...]
    for group in range(4):
        part = final[:, group * 128 : (group + 1) * 128]
        out_ref[:, group * 128 : (group + 1) * 128] = part.T.astype(jnp.bfloat16)


def attend(prefix_blocks, queries, own_keys, own_values, kv):
    vmem = pl.BlockSpec(memory_space=pltpu.VMEM)
    return pl.pallas_call(
        attend_kernel,
        out_shape=jax.ShapeDtypeStruct((128, 512), jnp.bfloat16),
        in_specs=[pl.BlockSpec(memory_space=pltpu.SMEM)] + [vmem] * 4,
        out_specs=vmem,
        scratch_shapes=[
            pltpu.VMEM((REACH + 1, BLOCK, 512), jnp.float32),
            pltpu.VMEM((1, 512), jnp.float32),
            pltpu.VMEM((1, 512), jnp.float32),
            pltpu.VMEM((HEAD_DIM, 512), jnp.float32),
        ],
        compiler_params=pltpu.CompilerParams(vmem_limit_bytes=24 * 1024 * 1024),
        name="attend",
    )(prefix_blocks, queries, own_keys, own_values, kv)


def on_device(slice_rows, w_query, w_key, w_value, prefix_keys, prefix_values, prefix_blocks):
    queries, own_keys, own_values, kv = gather(
        slice_rows, w_query, w_key, w_value, prefix_keys, prefix_values
    )
    return attend(prefix_blocks, queries, own_keys, own_values, kv)


def solution(mesh):
    in_specs = (
        P("section", "head"),
        P(None, "head"),
        P(None, "head"),
        P(None, "head"),
        P("section", "head"),
        P("section", "head"),
        P(),
    )
    out_specs = P("section", "head")
    return jax.shard_map(
        on_device, mesh=mesh, in_specs=in_specs, out_specs=out_specs, check_vma=False
    )
```

time: 111 us -> 36.8 us (0.33)
  the two profiles are of different devices: /device:TPU:207 before, /device:TPU:65 now
where the time goes in v2:
time: 36.8 us; the launch traced here: 36.5 us
  Pallas kernels  36.5 us (99%)
    pallas_call x1, Pallas kernels, gather(): pl.pallas_call(gather_kernel, out_shape=(pltpu.VMEM((512, HEAD_DIM), bf16...  32.6 us
    pallas_call x1, Pallas kernels, attend(): pl.pallas_call(attend_kernel, out_shape=jax.ShapeDtypeStruct((128, 512),...  3.83 us

profile of v2, /device:TPU:65, one launch (start us, length us, event | category | flops | bytes accessed | tf_op | source)
XLA Modules:
  0.0 36.5 jit_solution(12877315639674987594)
XLA Ops:
  0.0 0.0 copy-start
  0.0 32.6 %gather.1 = (bf16[512,128]{1,0:T(8,128)(2,1)S(1)}, bf16[128,128]{1,0:T(8,128)(2,1)S(1)}, bf16[128,128]{1,0:T(8,128)(2,1)S(1)}, bf16[9,2,512,128]{3,2,1,0:T(8,128)(2,1)S(1)}) custom-call(bf16[128,512]{1,0:T(8,128)(2,1)} %x_ref.1, bf16[4096,512]{1,0:T(8,128)(2,1)} %wq_ref.1, bf16[4096,128]{1,0:T(8,128)(2,1)} %wk_ref.1, bf16[4096,128]{1,0:T(8,128)(2,1)} %wv_ref.1, ...), custom_call_target="tpu_custom_call" | custom-call | tf_op jit(solution)/shard_map/gather/pallas_call | solution.py:541
  32.6 0.0 copy-done
  32.6 3.8 %attend.1 = bf16[128,512]{1,0:T(8,128)(2,1)} custom-call(s32[64]{0:T(128)S(1)} %copy-done, bf16[512,128]{1,0:T(8,128)(2,1)S(1)} %get-tuple-element.9.q_ref, bf16[128,128]{1,0:T(8,128)(2,1)S(1)} %get-tuple-element.10.k_ref, bf16[128,128]{1,0:T(8,128)(2,1)S(1)} %get-tuple-element.11.v_ref, bf16[9,2,512,128]{3,2,1,0:T(8,128)(2,1)S(1)} %get-tuple-element.12.kv_ref), custom_call_target="tpu_custom_call" | custom-call | tf_op jit(solution)/shard_map/attend/pallas_call | solution.py:638
Async XLA Ops:
  0.0 32.6 %copy-start = (s32[64]{0:T(128)S(1)}, s32[64]{0:T(128)}, u32[]{:S(2)}) copy-start(s32[64]{0:T(128)} %pb_ref.1) | copy-start | bytes 772
